TPU v7x, 128 devices: a whole 4x4x4 slice. The times are simulated.
128 devices in a mesh: tm: 16 (over z, y), col: 8 (over x, core).
Axes of the slice: x: 4, y: 4, z: 4, core: 2. Of those that a mesh axis runs over, the one named last changes fastest.
Arguments:
- block_values: bfloat16 [8, 32768, 128], P('col', 'tm'), may hold values from -6 to 6
- block_shifts: bfloat16 [8, 32768, 128], P('col', 'tm'), may hold values from -1 to 1
- block_sensor: int32 [8, 32768], P('col', 'tm'), may hold values from 0 to 2047
- block_window: int32 [8, 32768], P('col', 'tm'), may hold values from 0 to 3
- block_owner: int32 [8, 32768, 1], P('col', 'tm'), may hold values from 0 to 15; in each aligned block of 2048 rows (0 to 2047, 2048 to 4095, ..., all dimensions but the last counted through in order) at most 192 rows name the same one
- block_counts: int32 [8, 16], P('col', 'tm'), may hold values from 1536 to 2048
- calibration: bfloat16 [16384, 4096], P('tm', 'col'), may hold values from -0.046875 to 0.046875
Outputs:
- calibrated: bfloat16 [8192, 4096], P('tm', 'col')
Inputs may be any that keep to these rules, and one draw needn't show every extreme that they name: `block_owner`: among the 2048 block slots of one device, at most 192 name the same owner, a bound that some block reaches. The live blocks of device (tm t, col c) are its first block_counts[c, t] slots.
All inputs are finite; a program needn't handle non-finite values.
Results may differ from a plain program's by a relative error of at most 0.015.
Values may be sent and summed in bfloat16 or wider, within the bound.
A program may use at most 128 MiB of HBM per device.

v0:
```python
import jax
import jax.numpy as jnp
from jax import lax
from jax.sharding import Mesh
from jax.sharding import PartitionSpec as P

SENSORS = 16384
ROWS_DEV = 512
TM = ("tm_0", "tm_1")


def cut_rows(length, count):
    unit = 8 if length >= 8 * count else 1
    return [length // unit * k // count * unit for k in range(1, count)]


def gather_in_order(shard, axes, sequence):
    parts = shard[None]
    for k in sequence:
        parts = lax.all_gather(parts, axes[k], axis=0, tiled=True)
    carried = [lax.axis_size(axes[k]) for k in reversed(sequence)]
    parts = parts.reshape(*carried, *shard.shape)
    turned = sorted(range(len(sequence)), key=lambda place: sequence[len(sequence) - 1 - place])
    return parts.transpose(*turned, *range(len(sequence), parts.ndim)).reshape(-1, *shard.shape)


def joined_along(parts, dim):
    lengths = list(parts.shape[1:])
    lengths[dim] *= parts.shape[0]
    return jnp.moveaxis(parts, 0, dim).reshape(lengths)


def gather_all_axes(shard, axes, dim):
    numbers = list(range(len(axes)))[::-1]
    cut = shard.shape.index(max(shard.shape[:-1] or shard.shape))
    edges = [0, *cut_rows(shard.shape[cut], len(axes)), shard.shape[cut]]
    outs = []
    for k, (start, end) in enumerate(zip(edges, edges[1:])):
        if end > start:
            slab = lax.slice_in_dim(shard, start, end, axis=cut)
            outs.append(gather_in_order(slab, axes, numbers[k:] + numbers[:k]))
    return joined_along(jnp.concatenate(outs, axis=cut + 1), dim)


def spread_samples(values, shifts):
    samples = values.astype(jnp.float32)
    offsets = shifts.astype(jnp.float32)
    result = jnp.zeros(samples.shape, jnp.float32)
    lead = [(0, 0)] * (samples.ndim - 1)
    for displace in (-1, 0, 1):
        weight = jnp.maximum(0.0, 1.0 - jnp.abs(offsets - displace)).astype(jnp.bfloat16)
        weight = lax.optimization_barrier(weight).astype(jnp.float32)
        product = weight * samples
        if displace == 1:
            result = result + jnp.pad(product[..., :-1], lead + [(1, 0)])
        elif displace == -1:
            result = jnp.pad(product[..., 1:], lead + [(0, 1)])
        else:
            result = result + product
    return result


def spread_slots(moved_slots):
    return spread_samples(moved_slots[:, :, 0], moved_slots[:, :, 1])


def per_device(
    block_values, block_shifts, block_sensor, block_window, block_owner, block_counts, calibration
):
    values = block_values[0]
    shifts = block_shifts[0]
    blocks = values.shape[0]
    length = values.shape[1]
    owners = lax.axis_size(TM)
    group_size = SENSORS // lax.axis_size("col")
    windows = ROWS_DEV // length
    capacity = blocks * 3 // (2 * owners)
    slot_total = owners * capacity
    block_index = lax.iota(jnp.int32, blocks)
    is_live = block_index < block_counts[0, 0]
    values = jnp.where(is_live[:, None], values, jnp.zeros_like(values))
    owner_ids = block_owner[0, :, 0]
    owner_onehot = (owner_ids[:, None] == lax.iota(jnp.int32, owners)[None, :]).astype(jnp.bfloat16)
    lower_mask = (block_index[:, None] > block_index[None, :]).astype(jnp.bfloat16)
    earlier = jnp.dot(lower_mask, owner_onehot, preferred_element_type=jnp.float32)
    slot_rank = jnp.sum(earlier * owner_onehot.astype(jnp.float32), axis=1).astype(jnp.int32)
    slot_index = owner_ids * capacity + slot_rank
    slot_match = slot_index[None, :] == lax.iota(jnp.int32, slot_total)[:, None]
    source = jnp.max(jnp.where(slot_match, block_index[None, :], -1), axis=1)
    filled = source >= 0
    source_row = jnp.maximum(source, 0)
    row_keys = block_window[0] * group_size + block_sensor[0]
    payload = jnp.stack((values, shifts), axis=1)
    outgoing = jnp.where(
        filled[:, None, None], jnp.take(payload, source_row, axis=0), jnp.zeros((), jnp.bfloat16)
    )
    outgoing = outgoing.reshape(owners, capacity, 2, length)
    outgoing_keys = jnp.where(filled, jnp.take(row_keys, source_row, axis=0), 0).reshape(
        owners, capacity
    )
    contribution = spread_slots(
        lax.all_to_all(outgoing, TM, split_axis=0, concat_axis=0, tiled=True)
    )
    incoming_keys = lax.all_to_all(outgoing_keys, TM, split_axis=0, concat_axis=0, tiled=True)
    flat_keys = incoming_keys.reshape(-1)
    flat_contrib = contribution.reshape(-1, length)
    upper_part = flat_contrib.astype(jnp.bfloat16)
    lower_part = (flat_contrib - upper_part.astype(jnp.float32)).astype(jnp.bfloat16)
    sensor_iota = lax.iota(jnp.int32, group_size)
    window_rows = []
    for window in range(windows):
        target = flat_keys - window * group_size
        place_onehot = (target[:, None] == sensor_iota[None, :]).astype(jnp.bfloat16)
        dims = (((0,), (0,)), ((), ()))
        window_sum = lax.dot_general(
            upper_part, place_onehot, dims, preferred_element_type=jnp.float32
        )
        window_sum = window_sum + lax.dot_general(
            lower_part, place_onehot, dims, preferred_element_type=jnp.float32
        )
        window_rows.append(window_sum)
    aligned = jnp.concatenate(window_rows, axis=0).astype(jnp.bfloat16)
    cal_rows = gather_all_axes(calibration, TM, 0)
    running = jnp.dot(
        lax.all_gather(aligned, "col", axis=1, tiled=True),
        cal_rows,
        preferred_element_type=jnp.float32,
    )
    return running.astype(jnp.bfloat16)


def solution(mesh):
    torus = Mesh(mesh.devices.reshape(4, 4, mesh.shape["col"]), ("tm_0", "tm_1", "col"))
    in_specs = (
        P("col", TM, None),
        P("col", TM, None),
        P("col", TM),
        P("col", TM),
        P("col", TM, None),
        P("col", TM),
        P(TM, "col"),
    )
    out_specs = P(TM, "col")
    return jax.shard_map(
        per_device, mesh=torus, in_specs=in_specs, out_specs=out_specs, check_vma=False
    )
```

profile of v0, /device:TPU:1, one launch (start us, length us, event | category | flops | bytes accessed | tf_op | source)
XLA Modules:
  0.0 359.0 jit_solution(3384023761466500668)
XLA Ops:
  9.6 33.4 %all-gather.16.cloned.1.call-done = bf16[2048,512]{1,0:T(8,128)(2,1)} async-done(((bf16[512,512]{1,0:T(8,128)(2,1)}), bf16[2048,512]{1,0:T(8,128)(2,1)}) %all-gather.16.cloned.1.call-update) | async-done | bytes 2097168 | tf_op jit(solution)/shard_map/all_gather | solution.py:20
  43.2 32.3 %all-gather.14.cloned.1.call-done = bf16[2048,512]{1,0:T(8,128)(2,1)} async-done(((bf16[512,512]{1,0:T(8,128)(2,1)}), bf16[2048,512]{1,0:T(8,128)(2,1)}) %all-gather.14.cloned.1.call-update) | async-done | bytes 2097168 | tf_op jit(solution)/shard_map/all_gather | solution.py:20
  77.0 3.4 select_reduce_fusion
  80.4 17.4 %gather_fusion.1 = s32[3072]{0:T(1024)S(1)} fusion(s32[2048]{0:T(1024)S(1)} %bitcast.37, s32[3072]{0:T(1024)S(1)} %maximum_clamp_fusion), kind=kCustom, calls=%fused_computation.1 | custom fusion | bytes 36864 | tf_op jit(solution)/shard_map/jit(_take)/gather | solution.py:98
  98.5 5.7 %all-to-all-start.1 = ((s32[16,1,192]{2,1,0:T(1,128)}), s32[16,1,192]{2,1,0:T(1,128)S(1)}, u32[]{:S(2)}, u32[]{:S(2)}) async-start(s32[16,1,192]{2,1,0:T(1,128)} %select_n.64), calls=%async_computation.1 | async-start | bytes 32768 | tf_op jit(solution)/shard_map/all_to_all | solution.py:104
  105.0 8.1 %copy.20 = bf16[2048,1,128]{2,1,0:T(2,128)(2,1)S(1)} copy(bf16[2048,1,128]{2,0,1:T(8,128)(2,1)S(1)} %bitcast.46) | data formatting | bytes 1048576 | tf_op jit(solution)/shard_map/stack;squeeze | solution.py:93
  113.2 15.2 %broadcast_select_fusion.2 = bf16[2048,1,128]{2,1,0:T(2,128)(2,1)S(1)} fusion(pred[2048]{0:T(1024)(128)(4,1)S(1)} %iota_compare_fusion.37, bf16[2048,1,128]{2,0,1:T(8,128)(2,1)S(1)} %bitcast.47), kind=kLoop, calls=%fused_computation.42 | loop fusion | flops 262144 | bytes 1050624 | tf_op jit(solution)/shard_map/jit(_where)/select_n | solution.py:81
  130.8 10.4 %gather_fusion = bf16[3072,2,128]{2,1,0:T(2,128)(2,1)S(1)} fusion(bf16[2048,2,128]{2,1,0:T(2,128)(2,1)S(1)} %pad_maximum_fusion.2, s32[3072]{0:T(1024)S(1)} %maximum_clamp_fusion), kind=kCustom, calls=%fused_computation | custom fusion | bytes 3158016 | tf_op jit(solution)/shard_map/jit(_take)/gather | solution.py:95
  141.3 9.9 %broadcast_select_fusion.1 = bf16[16,192,2,128]{3,2,1,0:T(2,128)(2,1)} fusion(pred[16,192]{1,0:T(8,128)(4,1)S(1)} %ge.33, bf16[16,192,2,128]{3,2,1,0:T(2,128)(2,1)S(1)} %bitcast.43, pred[16,192]{1,0:T(8,128)(4,1)S(1)} %le.30), kind=kLoop, calls=%fused_computation.28 | loop fusion | flops 1572864 | bytes 3151872 | tf_op jit(solution)/shard_map/jit(_where)/select_n | solution.py:94
  151.2 6.7 %all-to-all-start = ((bf16[16,192,2,128]{3,2,1,0:T(2,128)(2,1)}), bf16[16,192,2,128]{3,2,1,0:T(2,128)(2,1)S(1)}, u32[]{:S(2)}, u32[]{:S(2)}) async-start(bf16[16,192,2,128]{3,2,1,0:T(2,128)(2,1)} %broadcast_select_fusion.1), calls=%async_computation | async-start | bytes 3145728 | tf_op jit(solution)/shard_map/all_to_all | solution.py:102
  158.2 20.8 %all-to-all-done = bf16[16,192,2,128]{3,2,1,0:T(2,128)(2,1)S(1)} async-done(((bf16[16,192,2,128]{3,2,1,0:T(2,128)(2,1)}), bf16[16,192,2,128]{3,2,1,0:T(2,128)(2,1)S(1)}, u32[]{:S(2)}, u32[]{:S(2)}) %all-to-all-start) | async-done | bytes 1572896 | tf_op jit(solution)/shard_map/all_to_all | solution.py:102
  184.0 5.3 %fusion.6 = f32[128,2048]{1,0:T(8,128)S(1)} fusion(bf16[3072,128]{1,0:T(8,128)(2,1)S(1)} %get-tuple-element.8, s32[3072]{0:T(1024)S(1)} %eq.36), kind=kOutput, calls=%fused_computation.12 | convolution fusion | flops 1616904192 | bytes 1847296 | tf_op jit(solution)/shard_map/dot_general | solution.py:118
  189.3 5.3 %fusion = f32[128,2048]{1,0:T(8,128)S(1)} fusion(bf16[3072,128]{1,0:T(8,128)(2,1)S(1)} %get-tuple-element.8, s32[3072]{0:T(1024)S(1)} %get-tuple-element.20), kind=kOutput, calls=%fused_computation.3 | convolution fusion | flops 1616904192 | bytes 1847296 | tf_op jit(solution)/shard_map/dot_general | solution.py:118
  194.7 5.5 %fusion.2 = f32[128,2048]{1,0:T(8,128)S(1)} fusion(bf16[3072,128]{1,0:T(8,128)(2,1)S(1)} %get-tuple-element.8, s32[3072]{0:T(1024)S(1)} %get-tuple-element.21), kind=kOutput, calls=%fused_computation.6 | convolution fusion | flops 1616904192 | bytes 1847296 | tf_op jit(solution)/shard_map/dot_general | solution.py:118
  200.2 5.3 %fusion.4 = f32[128,2048]{1,0:T(8,128)S(1)} fusion(bf16[3072,128]{1,0:T(8,128)(2,1)S(1)} %get-tuple-element.8, s32[3072]{0:T(1024)S(1)} %get-tuple-element.19), kind=kOutput, calls=%fused_computation.9 | convolution fusion | flops 1616904192 | bytes 1847296 | tf_op jit(solution)/shard_map/dot_general | solution.py:118
  205.5 5.5 %fusion.21 = bf16[128,2048]{1,0:T(8,128)(2,1)S(1)} fusion(f32[128,2048]{1,0:T(8,128)S(1)} %fusion, bf16[3072,128]{1,0:T(8,128)(2,1)S(1)} %get-tuple-element.9, s32[3072]{0:T(1024)S(1)} %get-tuple-element.20), kind=kOutput, calls=%fused_computation.33 | convolution fusion | flops 1617428480 | bytes 2371584 | tf_op jit(solution)/shard_map/dot_general | solution.py:115
  211.1 5.3 %fusion.22 = bf16[128,2048]{1,0:T(8,128)(2,1)S(1)} fusion(f32[128,2048]{1,0:T(8,128)S(1)} %fusion.2, bf16[3072,128]{1,0:T(8,128)(2,1)S(1)} %get-tuple-element.9, s32[3072]{0:T(1024)S(1)} %get-tuple-element.21), kind=kOutput, calls=%fused_computation.34 | convolution fusion | flops 1617428480 | bytes 2371584 | tf_op jit(solution)/shard_map/dot_general | solution.py:115
  216.4 5.3 %fusion.23 = bf16[128,2048]{1,0:T(8,128)(2,1)S(1)} fusion(f32[128,2048]{1,0:T(8,128)S(1)} %fusion.4, bf16[3072,128]{1,0:T(8,128)(2,1)S(1)} %get-tuple-element.9, s32[3072]{0:T(1024)S(1)} %get-tuple-element.19), kind=kOutput, calls=%fused_computation.35 | convolution fusion | flops 1617428480 | bytes 2371584 | tf_op jit(solution)/shard_map/dot_general | solution.py:115
  221.8 5.6 %fusion.24 = bf16[128,2048]{1,0:T(8,128)(2,1)S(1)} fusion(f32[128,2048]{1,0:T(8,128)S(1)} %fusion.6, bf16[3072,128]{1,0:T(8,128)(2,1)S(1)} %get-tuple-element.9, s32[3072]{0:T(1024)S(1)} %eq.36), kind=kOutput, calls=%fused_computation.36 | convolution fusion | flops 1617428480 | bytes 2371584 | tf_op jit(solution)/shard_map/dot_general | solution.py:115
  228.9 7.3 %copy.22 = bf16[4,4,512,512]{3,2,0,1:T(8,128)(2,1)} copy(bf16[4,4,512,512]{3,2,1,0:T(8,128)(2,1)} %bitcast.42) | data formatting | bytes 16777216 | tf_op jit(solution)/shard_map/reshape | solution.py:22
  236.2 11.4 %all-gather.10.cloned.1.call-done = bf16[16,512,512]{2,1,0:T(8,128)(2,1)} async-done(((bf16[4,512,512]{2,1,0:T(8,128)(2,1)}), bf16[16,512,512]{2,1,0:T(8,128)(2,1)}) %all-gather.10.cloned.1.call-update) | async-done | bytes 8388624 | tf_op jit(solution)/shard_map/all_gather | solution.py:20
  247.6 13.9 %pad_maximum_fusion = bf16[16,1024,512]{2,1,0:T(8,128)(2,1)} fusion(bf16[16,512,512]{2,1,0:T(8,128)(2,1)} %bitcast.38, bf16[16,512,512]{2,1,0:T(8,128)(2,1)} %all-gather.10.cloned.1.call-done), kind=kLoop, calls=%fused_computation.16 | loop fusion | flops 33554432 | bytes 33554432 | tf_op jit(solution)/shard_map/concatenate | solution.py:42
  261.5 72.7 %all-gather.8.cloned.1.call-done = bf16[512,16384]{1,0:T(8,128)(2,1)} async-done(((bf16[512,2048]{1,0:T(8,128)(2,1)}), bf16[512,16384]{1,0:T(8,128)(2,1)}) %all-gather.8.cloned.1.call-update) | async-done | bytes 16777232 | tf_op jit(solution)/shard_map/all_gather | solution.py:125
  334.1 17.9 %convolution_convert_fusion = bf16[512,512]{1,0:T(8,128)(2,1)} fusion(bf16[512,16384]{1,0:T(8,128)(2,1)} %all-gather.8.cloned.1.call-done, bf16[16384,512]{1,0:T(8,128)(2,1)} %bitcast.41), kind=kOutput, calls=%fused_computation.61 | convolution fusion | flops 8590196736 | bytes 34078720 | tf_op jit(solution)/shard_map/dot_general | solution.py:124
  (42 shorter events, 14.7 us)
Async XLA Ops:
  6.5 68.9 %copy-start.2 = (s32[1,2048,1]{1,2,0:T(1,128)S(1)}, s32[1,2048,1]{1,2,0:T(1,128)}, u32[]{:S(2)}) copy-start(s32[1,2048,1]{1,2,0:T(1,128)} %param.11) | copy-start | bytes 24580
  6.5 36.5 %all-gather.16.cloned.1.call-start = ((), (), s32[]{:S(2)}) async-start(), calls=%async_computation.6 | async-start | bytes 2621440 | tf_op jit(solution)/shard_map/all_gather | solution.py:20
  8.8 66.6 %all-gather.14.cloned.1.call-start = ((), (), s32[]{:S(2)}) async-start(), calls=%async_computation.5 | async-start | bytes 2621440 | tf_op jit(solution)/shard_map/all_gather | solution.py:20
  9.6 219.3 %all-gather.12.cloned.1.call-start = ((), (), s32[]{:S(2)}) async-start(), calls=%async_computation.4 | async-start | bytes 10485760 | tf_op jit(solution)/shard_map/all_gather | solution.py:20
  43.1 37.3 %copy-start.3 = (s32[1,2048]{1,0:T(1,128)S(1)}, s32[1,2048]{1,0:T(1,128)}, u32[]{:S(2)}) copy-start(s32[1,2048]{1,0:T(1,128)} %param.9) | copy-start | bytes 24580
  43.1 37.3 %copy-start.4 = (s32[1,2048]{1,0:T(1,128)S(1)}, s32[1,2048]{1,0:T(1,128)}, u32[]{:S(2)}) copy-start(s32[1,2048]{1,0:T(1,128)} %param.10) | copy-start | bytes 24580
  43.1 204.5 %all-gather.10.cloned.1.call-start = ((), (), s32[]{:S(2)}) async-start(), calls=%async_computation.3 | async-start | bytes 10485760 | tf_op jit(solution)/shard_map/all_gather | solution.py:20
  80.4 24.6 %copy-start = (bf16[1,2048,128]{2,1,0:T(8,128)(2,1)S(1)}, bf16[1,2048,128]{2,1,0:T(8,128)(2,1)}, u32[]{:S(2)}) copy-start(bf16[1,2048,128]{2,1,0:T(8,128)(2,1)} %param.8) | copy-start | bytes 1572868
  80.4 32.8 %copy-start.1 = (bf16[1,2048,128]{2,1,0:T(8,128)(2,1)S(1)}, bf16[1,2048,128]{2,1,0:T(8,128)(2,1)}, u32[]{:S(2)}) copy-start(bf16[1,2048,128]{2,1,0:T(8,128)(2,1)} %param.7) | copy-start | bytes 1572868
  98.5 52.7 %all-to-all-start.1 = ((s32[16,1,192]{2,1,0:T(1,128)}), s32[16,1,192]{2,1,0:T(1,128)S(1)}, u32[]{:S(2)}, u32[]{:S(2)}) async-start(s32[16,1,192]{2,1,0:T(1,128)} %select_n.64), calls=%async_computation.1 | async-start | bytes 32768 | tf_op jit(solution)/shard_map/all_to_all | solution.py:104
  151.2 27.7 %all-to-all-start = ((bf16[16,192,2,128]{3,2,1,0:T(2,128)(2,1)}), bf16[16,192,2,128]{3,2,1,0:T(2,128)(2,1)S(1)}, u32[]{:S(2)}, u32[]{:S(2)}) async-start(bf16[16,192,2,128]{3,2,1,0:T(2,128)(2,1)} %broadcast_select_fusion.1), calls=%async_computation | async-start | bytes 3145728 | tf_op jit(solution)/shard_map/all_to_all | solution.py:102
  158.0 176.2 %all-gather.8.cloned.1.call-start = ((), (), s32[]{:S(2)}) async-start(), calls=%async_computation.2 | async-start | bytes 18874368 | tf_op jit(solution)/shard_map/all_gather | solution.py:125
Sparse Core Ops, SparseCore 0:
  9.0 34.0 all-gather.15
  44.7 30.6 all-gather.13
  77.1 83.2 all-gather.11
  161.9 85.6 all-gather.9
  249.1 84.9 all-gather.7
where the time goes:
time: 364 us; the launch traced here: 359 us
  waiting for transfers between devices  171 us (47%)
  matrix products  62.6 us (17%)
  other arithmetic  51.4 us (14%)
  local copies, waits for them, and re-layouts  46.6 us (13%)
  between operations  14.5 us (4%)
  starting transfers between devices  12.6 us (3%)
    all_gather x4, waiting for transfers between devices, gather_in_order(): parts = lax.all_gather(parts, axes[k], axis=0, tiled=True)  77.1 us
    all_gather x1, waiting for transfers between devices, per_device(): lax.all_gather(aligned, 'col', axis=1, tiled=True)  72.7 us
    dot_general x4, matrix products, per_device(): lax.dot_general(upper_part, place_onehot, dims, preferred_element_type=jn...  21.8 us
    dot_general x4, matrix products, per_device(): lax.dot_general(lower_part, place_onehot, dims, preferred_element_type=jn...  21.5 us
    all_to_all x1, waiting for transfers between devices, per_device(): lax.all_to_all(outgoing, TM, split_axis=0, concat_axis=0, tiled=True)  20.8 us
    dot_general x1, matrix products, per_device(): jnp.dot(lax.all_gather(aligned, 'col', axis=1, tiled=True), cal_rows, pre...  17.9 us
    gather x1, local copies, waits for them, and re-layouts, per_device(): jnp.take(row_keys, source_row, axis=0)  17.4 us
    select_n x1, other arithmetic, per_device(): values = jnp.where(is_live[:, None], values, jnp.zeros_like(values))  15.2 us
  transfers between devices with their start and end apart: 7, of which 5 were waited for; matrix products, arithmetic and copies ran while one was open for 39% of the time, Pallas kernels for 0%

commit v1 on v0

--- a/solution.py
+++ b/solution.py
@@ -7,6 +7,11 @@
 SENSORS = 16384
 ROWS_DEV = 512
 TM = ("tm_0", "tm_1")
+
+
+def swapped_in(x, axis, dim):
+    sent = jnp.stack([x] * lax.axis_size(axis))
+    return jnp.concatenate(lax.all_to_all(sent, axis, 0, 0), axis=dim)
 
 
 def cut_rows(length, count):
@@ -121,11 +126,7 @@
         window_rows.append(window_sum)
     aligned = jnp.concatenate(window_rows, axis=0).astype(jnp.bfloat16)
     cal_rows = gather_all_axes(calibration, TM, 0)
-    running = jnp.dot(
-        lax.all_gather(aligned, "col", axis=1, tiled=True),
-        cal_rows,
-        preferred_element_type=jnp.float32,
-    )
+    running = jnp.dot(swapped_in(aligned, "col", 1), cal_rows, preferred_element_type=jnp.float32)
     return running.astype(jnp.bfloat16)
 
 

time: 364 us -> 445 us (1.22)
  waiting for transfers between devices: 171 us -> 236 us
  local copies, waits for them, and re-layouts: 46.6 us -> 55.3 us
  starting transfers between devices: 12.6 us -> 20.4 us
    all_to_all x0 -> x1, waiting for transfers between devices: none -> 87.8 us  [swapped_in(): return jnp.concatenate(lax.all_to_all(sent, axis, 0, 0), axis=dim)]
    all_gather x1 -> x0, waiting for transfers between devices: 72.7 us -> none  [per_device(): lax.all_gather(aligned, 'col', axis=1, tiled=True)]
    all_gather x4, waiting for transfers between devices: 77.1 us -> 108 us  [gather_in_order(): parts = lax.all_gather(parts, axes[k], axis=0, tiled=True)]
    all_to_all x1, waiting for transfers between devices: 20.8 us -> 39.5 us  [per_device(): lax.all_to_all(outgoing, TM, split_axis=0, concat_axis=0, tiled=True)]
    all_to_all x0 -> x1, starting transfers between devices: none -> 8.04 us  [swapped_in(): return jnp.concatenate(lax.all_to_all(sent, axis, 0, 0), axis=dim)]
    another operation x0 -> x1, local copies, waits for them, and re-layouts: none -> 5.93 us  [swapped_in(): sent = jnp.stack([x] * lax.axis_size(axis))]
  transfers between devices with their start and end apart: 7 -> 7, of which waited for: 5 -> 4; matrix products, arithmetic and copies ran while one was open for 39% -> 34% of each run, Pallas kernels for 0% -> 0%
where the time goes in v1:
time: 445 us; the launch traced here: 440 us
  waiting for transfers between devices  236 us (53%)
  matrix products  62.8 us (14%)
  local copies, waits for them, and re-layouts  55.3 us (12%)
  other arithmetic  51.2 us (12%)
  starting transfers between devices  20.4 us (5%)
  between operations  14.5 us (3%)
    all_gather x4, waiting for transfers between devices, gather_in_order(): parts = lax.all_gather(parts, axes[k], axis=0, tiled=True)  108 us
    all_to_all x1, waiting for transfers between devices, swapped_in(): return jnp.concatenate(lax.all_to_all(sent, axis, 0, 0), axis=dim)  87.8 us
    all_to_all x1, waiting for transfers between devices, per_device(): lax.all_to_all(outgoing, TM, split_axis=0, concat_axis=0, tiled=True)  39.5 us
    dot_general x4, matrix products, per_device(): lax.dot_general(upper_part, place_onehot, dims, preferred_element_type=jn...  21.8 us
    dot_general x4, matrix products, per_device(): lax.dot_general(lower_part, place_onehot, dims, preferred_element_type=jn...  21.5 us
    dot_general x1, matrix products, per_device(): jnp.dot(swapped_in(aligned, 'col', 1), cal_rows, preferred_element_type=j...  18 us
    gather x1, local copies, waits for them, and re-layouts, per_device(): jnp.take(row_keys, source_row, axis=0)  17.4 us
    select_n x1, other arithmetic, per_device(): values = jnp.where(is_live[:, None], values, jnp.zeros_like(values))  15.2 us
  transfers between devices with their start and end apart: 7, of which 4 were waited for; matrix products, arithmetic and copies ran while one was open for 34% of the time, Pallas kernels for 0%

profile of v1, /device:TPU:1, one launch (start us, length us, event | category | flops | bytes accessed | tf_op | source)
XLA Modules:
  0.0 440.5 jit_solution(9491405579640920867)
XLA Ops:
  9.6 33.4 %all-gather.13.cloned.1.call-done = bf16[2048,512]{1,0:T(8,128)(2,1)} async-done(((bf16[512,512]{1,0:T(8,128)(2,1)}), bf16[2048,512]{1,0:T(8,128)(2,1)}) %all-gather.13.cloned.1.call-update) | async-done | bytes 2097168 | tf_op jit(solution)/shard_map/all_gather | solution.py:25
  48.1 17.4 %gather_fusion.1 = s32[3072]{0:T(1024)S(1)} fusion(s32[2048]{0:T(1024)S(1)} %bitcast.40, s32[3072]{0:T(1024)S(1)} %maximum_clamp_fusion), kind=kCustom, calls=%fused_computation.1 | custom fusion | bytes 36864 | tf_op jit(solution)/shard_map/jit(_take)/gather | solution.py:103
  66.2 5.5 %all-to-all-start.1 = ((s32[16,1,192]{2,1,0:T(1,128)}), s32[16,1,192]{2,1,0:T(1,128)S(1)}, u32[]{:S(2)}, u32[]{:S(2)}) async-start(s32[16,1,192]{2,1,0:T(1,128)} %select_n.64), calls=%async_computation.1 | async-start | bytes 32768 | tf_op jit(solution)/shard_map/all_to_all | solution.py:109
  72.6 8.1 %copy.23 = bf16[2048,1,128]{2,1,0:T(2,128)(2,1)S(1)} copy(bf16[2048,1,128]{2,0,1:T(8,128)(2,1)S(1)} %bitcast.49) | data formatting | bytes 1048576 | tf_op jit(solution)/shard_map/stack;squeeze | solution.py:98
  80.7 15.2 %broadcast_select_fusion.2 = bf16[2048,1,128]{2,1,0:T(2,128)(2,1)S(1)} fusion(pred[2048]{0:T(1024)(128)(4,1)S(1)} %iota_compare_fusion.37, bf16[2048,1,128]{2,0,1:T(8,128)(2,1)S(1)} %bitcast.50), kind=kLoop, calls=%fused_computation.42 | loop fusion | flops 262144 | bytes 1050624 | tf_op jit(solution)/shard_map/jit(_where)/select_n | solution.py:86
  98.4 10.4 %gather_fusion = bf16[3072,2,128]{2,1,0:T(2,128)(2,1)S(1)} fusion(bf16[2048,2,128]{2,1,0:T(2,128)(2,1)S(1)} %pad_maximum_fusion.2, s32[3072]{0:T(1024)S(1)} %maximum_clamp_fusion), kind=kCustom, calls=%fused_computation | custom fusion | bytes 3158016 | tf_op jit(solution)/shard_map/jit(_take)/gather | solution.py:100
  108.8 10.0 %broadcast_select_fusion.1 = bf16[16,192,2,128]{3,2,1,0:T(2,128)(2,1)} fusion(pred[16,192]{1,0:T(8,128)(4,1)S(1)} %ge.33, bf16[16,192,2,128]{3,2,1,0:T(2,128)(2,1)S(1)} %bitcast.46, pred[16,192]{1,0:T(8,128)(4,1)S(1)} %le.30), kind=kLoop, calls=%fused_computation.28 | loop fusion | flops 1572864 | bytes 3151872 | tf_op jit(solution)/shard_map/jit(_where)/select_n | solution.py:99
  118.7 6.8 %all-to-all-start = ((bf16[16,192,2,128]{3,2,1,0:T(2,128)(2,1)}), bf16[16,192,2,128]{3,2,1,0:T(2,128)(2,1)S(1)}, u32[]{:S(2)}, u32[]{:S(2)}) async-start(bf16[16,192,2,128]{3,2,1,0:T(2,128)(2,1)} %broadcast_select_fusion.1), calls=%async_computation | async-start | bytes 3145728 | tf_op jit(solution)/shard_map/all_to_all | solution.py:107
  125.6 39.5 %all-to-all-done = bf16[16,192,2,128]{3,2,1,0:T(2,128)(2,1)S(1)} async-done(((bf16[16,192,2,128]{3,2,1,0:T(2,128)(2,1)}), bf16[16,192,2,128]{3,2,1,0:T(2,128)(2,1)S(1)}, u32[]{:S(2)}, u32[]{:S(2)}) %all-to-all-start) | async-done | bytes 1572896 | tf_op jit(solution)/shard_map/all_to_all | solution.py:107
  170.2 5.3 %fusion.6 = f32[128,2048]{1,0:T(8,128)S(1)} fusion(bf16[3072,128]{1,0:T(8,128)(2,1)S(1)} %get-tuple-element.8, s32[3072]{0:T(1024)S(1)} %eq.36), kind=kOutput, calls=%fused_computation.12 | convolution fusion | flops 1616904192 | bytes 1847296 | tf_op jit(solution)/shard_map/dot_general | solution.py:123
  175.5 5.3 %fusion.4 = f32[128,2048]{1,0:T(8,128)S(1)} fusion(bf16[3072,128]{1,0:T(8,128)(2,1)S(1)} %get-tuple-element.8, s32[3072]{0:T(1024)S(1)} %get-tuple-element.19), kind=kOutput, calls=%fused_computation.9 | convolution fusion | flops 1616904192 | bytes 1847296 | tf_op jit(solution)/shard_map/dot_general | solution.py:123
  180.9 5.5 %fusion.2 = f32[128,2048]{1,0:T(8,128)S(1)} fusion(bf16[3072,128]{1,0:T(8,128)(2,1)S(1)} %get-tuple-element.8, s32[3072]{0:T(1024)S(1)} %get-tuple-element.21), kind=kOutput, calls=%fused_computation.6 | convolution fusion | flops 1616904192 | bytes 1847296 | tf_op jit(solution)/shard_map/dot_general | solution.py:123
  186.4 5.3 %fusion = f32[128,2048]{1,0:T(8,128)S(1)} fusion(bf16[3072,128]{1,0:T(8,128)(2,1)S(1)} %get-tuple-element.8, s32[3072]{0:T(1024)S(1)} %get-tuple-element.20), kind=kOutput, calls=%fused_computation.3 | convolution fusion | flops 1616904192 | bytes 1847296 | tf_op jit(solution)/shard_map/dot_general | solution.py:123
  191.7 5.5 %fusion.24 = bf16[128,2048]{1,0:T(8,128)(2,1)S(1)} fusion(f32[128,2048]{1,0:T(8,128)S(1)} %fusion.6, bf16[3072,128]{1,0:T(8,128)(2,1)S(1)} %get-tuple-element.9, s32[3072]{0:T(1024)S(1)} %eq.36), kind=kOutput, calls=%fused_computation.36 | convolution fusion | flops 1617428480 | bytes 2371584 | tf_op jit(solution)/shard_map/dot_general | solution.py:120
  197.3 5.3 %fusion.23 = bf16[128,2048]{1,0:T(8,128)(2,1)S(1)} fusion(f32[128,2048]{1,0:T(8,128)S(1)} %fusion.4, bf16[3072,128]{1,0:T(8,128)(2,1)S(1)} %get-tuple-element.9, s32[3072]{0:T(1024)S(1)} %get-tuple-element.19), kind=kOutput, calls=%fused_computation.35 | convolution fusion | flops 1617428480 | bytes 2371584 | tf_op jit(solution)/shard_map/dot_general | solution.py:120
  202.6 5.3 %fusion.22 = bf16[128,2048]{1,0:T(8,128)(2,1)S(1)} fusion(f32[128,2048]{1,0:T(8,128)S(1)} %fusion.2, bf16[3072,128]{1,0:T(8,128)(2,1)S(1)} %get-tuple-element.9, s32[3072]{0:T(1024)S(1)} %get-tuple-element.21), kind=kOutput, calls=%fused_computation.34 | convolution fusion | flops 1617428480 | bytes 2371584 | tf_op jit(solution)/shard_map/dot_general | solution.py:120
  208.0 5.6 %fusion.21 = bf16[128,2048]{1,0:T(8,128)(2,1)S(1)} fusion(f32[128,2048]{1,0:T(8,128)S(1)} %fusion, bf16[3072,128]{1,0:T(8,128)(2,1)S(1)} %get-tuple-element.9, s32[3072]{0:T(1024)S(1)} %get-tuple-element.20), kind=kOutput, calls=%fused_computation.33 | convolution fusion | flops 1617428480 | bytes 2371584 | tf_op jit(solution)/shard_map/dot_general | solution.py:120
  217.9 5.9 %stack.5 = bf16[8,512,2048]{1,2,0:T(8,128)(2,1)} broadcast(bf16[512,2048]{0,1:T(8,128)(2,1)S(1)} %copy.25), dimensions={1,2} | broadcast | bytes 18874368 | tf_op jit(solution)/shard_map/stack | solution.py:13
  223.8 8.0 %all-to-all-start.2 = ((bf16[8,512,2048]{1,2,0:T(8,128)(2,1)}), bf16[8,512,2048]{1,2,0:T(8,128)(2,1)}, u32[]{:S(2)}, u32[]{:S(2)}) async-start(bf16[8,512,2048]{1,2,0:T(8,128)(2,1)} %stack.5), calls=%async_computation.2 | async-start | bytes 33554432 | tf_op jit(solution)/shard_map/all_to_all | solution.py:14
  232.5 7.3 %copy.26 = bf16[4,4,512,512]{3,2,0,1:T(8,128)(2,1)} copy(bf16[4,4,512,512]{3,2,1,0:T(8,128)(2,1)} %bitcast.45) | data formatting | bytes 16777216 | tf_op jit(solution)/shard_map/reshape | solution.py:27
  239.8 74.4 %all-gather.7.cloned.1.call-done = bf16[16,512,512]{2,1,0:T(8,128)(2,1)} async-done(((bf16[4,512,512]{2,1,0:T(8,128)(2,1)}), bf16[16,512,512]{2,1,0:T(8,128)(2,1)}) %all-gather.7.cloned.1.call-update) | async-done | bytes 8388624 | tf_op jit(solution)/shard_map/all_gather | solution.py:25
  314.2 13.6 %pad_maximum_fusion = bf16[16,1024,512]{2,1,0:T(8,128)(2,1)} fusion(bf16[16,512,512]{2,1,0:T(8,128)(2,1)} %bitcast.41, bf16[16,512,512]{2,1,0:T(8,128)(2,1)} %all-gather.7.cloned.1.call-done), kind=kLoop, calls=%fused_computation.16 | loop fusion | flops 33554432 | bytes 33554432 | tf_op jit(solution)/shard_map/concatenate | solution.py:47
  327.8 87.8 %all-to-all-done.2 = bf16[8,512,2048]{1,2,0:T(8,128)(2,1)} async-done(((bf16[8,512,2048]{1,2,0:T(8,128)(2,1)}), bf16[8,512,2048]{1,2,0:T(8,128)(2,1)}, u32[]{:S(2)}, u32[]{:S(2)}) %all-to-all-start.2) | async-done | bytes 16777248 | tf_op jit(solution)/shard_map/all_to_all | solution.py:14
  415.5 18.0 %convolution_convert_fusion = bf16[512,512]{1,0:T(8,128)(2,1)} fusion(bf16[512,16384]{0,1:T(8,128)(2,1)} %bitcast.12, bf16[16384,512]{1,0:T(8,128)(2,1)} %bitcast.44), kind=kOutput, calls=%fused_computation.61 | convolution fusion | flops 8590196736 | bytes 34078720 | tf_op jit(solution)/shard_map/dot_general | solution.py:129
  (43 shorter events, 21.4 us)
Async XLA Ops:
  6.5 36.5 %copy-start.2 = (s32[1,2048,1]{1,2,0:T(1,128)S(1)}, s32[1,2048,1]{1,2,0:T(1,128)}, u32[]{:S(2)}) copy-start(s32[1,2048,1]{1,2,0:T(1,128)} %param.11) | copy-start | bytes 24580
  6.5 36.5 %all-gather.13.cloned.1.call-start = ((), (), s32[]{:S(2)}) async-start(), calls=%async_computation.6 | async-start | bytes 2621440 | tf_op jit(solution)/shard_map/all_gather | solution.py:25
  8.8 223.1 %all-gather.11.cloned.1.call-start = ((), (), s32[]{:S(2)}) async-start(), calls=%async_computation.5 | async-start | bytes 2621440 | tf_op jit(solution)/shard_map/all_gather | solution.py:25
  8.9 39.1 %copy-start.3 = (s32[1,2048]{1,0:T(1,128)S(1)}, s32[1,2048]{1,0:T(1,128)}, u32[]{:S(2)}) copy-start(s32[1,2048]{1,0:T(1,128)} %param.9) | copy-start | bytes 24580
  8.9 39.1 %copy-start.4 = (s32[1,2048]{1,0:T(1,128)S(1)}, s32[1,2048]{1,0:T(1,128)}, u32[]{:S(2)}) copy-start(s32[1,2048]{1,0:T(1,128)} %param.10) | copy-start | bytes 24580
  9.6 222.9 %all-gather.9.cloned.1.call-start = ((), (), s32[]{:S(2)}) async-start(), calls=%async_computation.4 | async-start | bytes 10485760 | tf_op jit(solution)/shard_map/all_gather | solution.py:25
  48.1 24.5 %copy-start = (bf16[1,2048,128]{2,1,0:T(8,128)(2,1)S(1)}, bf16[1,2048,128]{2,1,0:T(8,128)(2,1)}, u32[]{:S(2)}) copy-start(bf16[1,2048,128]{2,1,0:T(8,128)(2,1)} %param.8) | copy-start | bytes 1572868
  48.1 32.7 %copy-start.1 = (bf16[1,2048,128]{2,1,0:T(8,128)(2,1)S(1)}, bf16[1,2048,128]{2,1,0:T(8,128)(2,1)}, u32[]{:S(2)}) copy-start(bf16[1,2048,128]{2,1,0:T(8,128)(2,1)} %param.7) | copy-start | bytes 1572868
  66.2 52.5 %all-to-all-start.1 = ((s32[16,1,192]{2,1,0:T(1,128)}), s32[16,1,192]{2,1,0:T(1,128)S(1)}, u32[]{:S(2)}, u32[]{:S(2)}) async-start(s32[16,1,192]{2,1,0:T(1,128)} %select_n.64), calls=%async_computation.1 | async-start | bytes 32768 | tf_op jit(solution)/shard_map/all_to_all | solution.py:109
  118.7 46.4 %all-to-all-start = ((bf16[16,192,2,128]{3,2,1,0:T(2,128)(2,1)}), bf16[16,192,2,128]{3,2,1,0:T(2,128)(2,1)S(1)}, u32[]{:S(2)}, u32[]{:S(2)}) async-start(bf16[16,192,2,128]{3,2,1,0:T(2,128)(2,1)} %broadcast_select_fusion.1), calls=%async_computation | async-start | bytes 3145728 | tf_op jit(solution)/shard_map/all_to_all | solution.py:107
  223.8 191.7 %all-to-all-start.2 = ((bf16[8,512,2048]{1,2,0:T(8,128)(2,1)}), bf16[8,512,2048]{1,2,0:T(8,128)(2,1)}, u32[]{:S(2)}, u32[]{:S(2)}) async-start(bf16[8,512,2048]{1,2,0:T(8,128)(2,1)} %stack.5), calls=%async_computation.2 | async-start | bytes 33554432 | tf_op jit(solution)/shard_map/all_to_all | solution.py:14
  231.9 82.3 %all-gather.7.cloned.1.call-start = ((), (), s32[]{:S(2)}) async-start(), calls=%async_computation.3 | async-start | bytes 10485760 | tf_op jit(solution)/shard_map/all_gather | solution.py:25
Sparse Core Ops, SparseCore 0:
  9.0 34.0 all-gather.12
  44.7 30.6 all-gather.10
  77.1 100.0 all-gather.8
  234.0 80.1 all-gather.6
